TPU v7x, 32 devices: a whole 2x2x4 slice. The times are simulated.
32 devices in a mesh: ctx: 16 (over z, y, x), tp: 2 (over core).
Axes of the slice: x: 2, y: 2, z: 4, core: 2. Of those that a mesh axis runs over, the one named last changes fastest.
Arguments:
- byte_states: bfloat16 [4096, 1024], P('ctx'), may hold values from -12 to 12, as said below
- patch_of_byte: int32 [4096], P('ctx'), may hold values from 0 to 125, as said below
- patch_first: int32 [16], replicated, may hold values from 0 to 991, as said below
- moved: int32 [2, 16], replicated, may hold values from 0 to 32, as said below
- w_qkv: bfloat16 [3, 1024, 2048], P(None, None, 'tp'), may hold values from -0.25 to 0.25, as said below
- d_attn: bfloat16 [1024, 2048], P('ctx', 'tp'), may hold values from -6 to 6
Outputs:
- attn_out: bfloat16 [1024, 2048], P('ctx', 'tp')
- byte_grad: bfloat16 [4096, 1024], P('ctx', 'tp')
Inputs may be any that keep to these rules, and one draw needn't show every extreme that they name: `patch_of_byte`: within each byte shard the numbers start at 0 and rise by 0 or 1 from byte to byte; a shard holds at most 126 patches, reached on some shard. `patch_first`: the sum of the patch counts of all earlier byte shards; shard 0 starts at 0. moved[0, 0] = 0 and moved[1, 15] = 0; every other entry is 1 to 32; every patch shard thereby receives exactly 64 patches, and the patch counts agree with patch_first and patch_of_byte. `w_qkv`: independent entries of order 1024 ** -0.5. `byte_states`: entries of order one.
All inputs are finite; a program needn't handle non-finite values.
Results may differ from a plain program's by a relative error of at most 0.011.
Values may be sent and summed in bfloat16 or wider, within the bound.
A program may use at most 64 MiB of HBM per device.

v0:
```python
import jax
import jax.numpy as jnp
from jax import lax
from jax.sharding import PartitionSpec as P

HD = 128


def extended_2(x, sides, width):
    for axis, dim in sides:
        peers, length = (lax.axis_size(axis), x.shape[dim])
        up = [(i, (i + 1) % peers) for i in range(peers - 1)]
        down = [(j, i) for i, j in up]
        last = lax.slice_in_dim(x, length - width, length, axis=dim)
        first = lax.slice_in_dim(x, 0, width, axis=dim)
        before = lax.ppermute(last, axis, up)
        after = lax.ppermute(first, axis, down)
        x = jnp.concatenate([before, x, after], axis=dim)
    return x


def pick_own(values, index):
    return lax.dynamic_index_in_dim(values, index, 0, keepdims=False)


def shards(byte_states, patch_of_byte, patch_first, moved, w_qkv, d_attn):
    ctx_index = lax.axis_index("ctx")
    n_ctx = lax.axis_size("ctx")
    rows = d_attn.shape[0]
    feats = d_attn.shape[1]
    heads = feats // HD
    capacity = 2 * rows
    total = rows * n_ctx
    scale = HD ** (-0.5)
    ends = jnp.concatenate([patch_first[1:], jnp.full((1,), total, jnp.int32)])
    counts = ends - patch_first
    lower_moves = moved[0]
    upper_moves = moved[1]
    zero_one = jnp.zeros((1,), jnp.int32)
    below_high = jnp.concatenate([zero_one, upper_moves[:-1]])
    above_low = jnp.concatenate([lower_moves[1:], zero_one])
    prev_first = jnp.concatenate([zero_one, patch_first[:-1]])
    prev_count = jnp.concatenate([zero_one, counts[:-1]])
    ranks = jnp.arange(rows, dtype=jnp.int32)[None, :]
    from_low = ranks < below_high[:, None]
    from_high = ranks >= (rows - above_low)[:, None]
    lower_local = prev_count[:, None] - below_high[:, None] + ranks
    own_local = lower_moves[:, None] + ranks - below_high[:, None]
    upper_local = ranks - (rows - above_low)[:, None]
    ids_all = jnp.where(
        from_low,
        prev_first[:, None] + lower_local,
        jnp.where(from_high, ends[:, None] + upper_local, patch_first[:, None] + own_local),
    )
    source_all = jnp.where(
        from_low,
        lower_local,
        jnp.where(from_high, 2 * capacity + upper_local, capacity + own_local),
    )
    wanted = pick_own(ids_all, ctx_index)
    source_rows = pick_own(source_all, ctx_index)
    key_place = ids_all.reshape(-1)
    slots = jnp.arange(capacity, dtype=jnp.int32)
    member = patch_of_byte[None, :] == slots[:, None]
    lengths = jnp.sum(member.astype(jnp.float32), axis=1)
    onehot = member.astype(jnp.bfloat16)
    part = byte_states.shape[1] // lax.axis_size("tp")
    source = lax.dynamic_slice_in_dim(byte_states, lax.axis_index("tp") * part, part, 1)
    pooled_local = (
        jnp.dot(onehot, source, preferred_element_type=jnp.float32)
        / jnp.maximum(lengths, 1.0)[:, None]
    ).astype(jnp.bfloat16)
    extended = extended_2(pooled_local, (("ctx", 0),), capacity)
    picker = (source_rows[:, None] == jnp.arange(3 * capacity, dtype=jnp.int32)[None, :]).astype(
        jnp.bfloat16
    )
    pooled = jnp.dot(picker, extended, preferred_element_type=jnp.float32).astype(jnp.bfloat16)
    pooled = lax.all_gather(pooled, "tp", axis=1, tiled=True)
    query = jnp.dot(pooled, w_qkv[0], preferred_element_type=jnp.float32).astype(jnp.bfloat16)
    keyed = jnp.dot(pooled, w_qkv[1], preferred_element_type=jnp.float32).astype(jnp.bfloat16)
    valued = jnp.dot(pooled, w_qkv[2], preferred_element_type=jnp.float32).astype(jnp.bfloat16)
    keys_all, values_all = (
        lax.all_gather(keyed, "ctx", axis=0, tiled=True),
        lax.all_gather(valued, "ctx", axis=0, tiled=True),
    )
    query3 = query.reshape(rows, heads, HD)
    keys3 = keys_all.reshape(total, heads, HD)
    values3 = values_all.reshape(total, heads, HD)
    causal = (wanted[:, None] >= key_place[None, :])[None, :, :]
    score = jnp.einsum("qhd,khd->hqk", query3, keys3, preferred_element_type=jnp.float32) * scale
    masked = jnp.where(causal, score, -jnp.inf)
    top = jnp.max(masked, axis=2, keepdims=True)
    lse = top + jnp.log(jnp.sum(jnp.exp(masked - top), axis=2, keepdims=True))
    prob = jnp.exp(jnp.where(causal, score - lse, -jnp.inf))
    probs = prob.astype(jnp.bfloat16)
    output3 = jnp.einsum("hqk,khd->qhd", probs, values3, preferred_element_type=jnp.float32).astype(
        jnp.bfloat16
    )
    attn_out = output3.reshape(rows, feats)
    grad3 = d_attn.reshape(rows, heads, HD)
    delta = jnp.sum(grad3.astype(jnp.float32) * output3.astype(jnp.float32), axis=2)
    dprob = jnp.einsum("qhd,khd->hqk", grad3, values3, preferred_element_type=jnp.float32)
    dscore = (prob * (dprob - jnp.transpose(delta)[:, :, None])).astype(jnp.bfloat16)
    d_query = (
        jnp.einsum("hqk,khd->qhd", dscore, keys3, preferred_element_type=jnp.float32) * scale
    ).astype(jnp.bfloat16)
    lse_rows = jnp.transpose(lse[:, :, 0])
    lse_all, delta_all = (
        lax.all_gather(lse_rows, "ctx", axis=0, tiled=True),
        lax.all_gather(delta, "ctx", axis=0, tiled=True),
    )
    own_keys = keyed.reshape(rows, heads, HD)
    own_values = valued.reshape(rows, heads, HD)
    q_piece = lax.all_gather(query, "ctx", axis=0, tiled=True)
    g_piece = lax.all_gather(d_attn, "ctx", axis=0, tiled=True)
    count = q_piece.shape[0]
    q_three = q_piece.reshape(count, heads, HD)
    g_three = g_piece.reshape(count, heads, HD)
    lse_piece = jnp.transpose(lse_all)
    delta_piece = jnp.transpose(delta_all)
    allowed = (key_place[:, None] >= wanted[None, :])[None, :, :]
    part_score = (
        jnp.einsum("qhd,khd->hqk", q_three, own_keys, preferred_element_type=jnp.float32) * scale
    )
    part_prob = jnp.exp(jnp.where(allowed, part_score - lse_piece[:, :, None], -jnp.inf))
    part_probs = part_prob.astype(jnp.bfloat16)
    d_value_sum = jnp.einsum(
        "hqk,qhd->khd", part_probs, g_three, preferred_element_type=jnp.float32
    )
    part_dprob = jnp.einsum("qhd,khd->hqk", g_three, own_values, preferred_element_type=jnp.float32)
    part_dscore = (part_prob * (part_dprob - delta_piece[:, :, None])).astype(jnp.bfloat16)
    d_key_sum = (
        jnp.einsum("hqk,qhd->khd", part_dscore, q_three, preferred_element_type=jnp.float32) * scale
    )
    d_key_sum, d_value_sum = (d_key_sum, d_value_sum)
    d_key = d_key_sum.astype(jnp.bfloat16).reshape(rows, feats)
    d_value = d_value_sum.astype(jnp.bfloat16).reshape(rows, feats)
    d_query = d_query.reshape(rows, feats)
    contract = (((1,), (1,)), ((), ()))
    partial_value = lax.dot_general(d_query, w_qkv[0], contract, preferred_element_type=jnp.float32)
    partial_value = partial_value + lax.dot_general(
        d_key, w_qkv[1], contract, preferred_element_type=jnp.float32
    )
    partial_value = partial_value + lax.dot_general(
        d_value, w_qkv[2], contract, preferred_element_type=jnp.float32
    )
    d_pooled = lax.psum_scatter(partial_value, "tp", scatter_dimension=1, tiled=True).astype(
        jnp.bfloat16
    )
    returned = extended_2(d_pooled, (("ctx", 0),), rows)
    my_count = pick_own(counts, ctx_index)
    my_low = pick_own(lower_moves, ctx_index)
    my_high = pick_own(upper_moves, ctx_index)
    my_below = pick_own(below_high, ctx_index)
    target = jnp.where(
        patch_of_byte < my_low,
        rows - my_low + patch_of_byte,
        jnp.where(
            patch_of_byte >= my_count - my_high,
            2 * rows + patch_of_byte - (my_count - my_high),
            rows + my_below + patch_of_byte - my_low,
        ),
    )
    chooser = (target[:, None] == jnp.arange(3 * rows, dtype=jnp.int32)[None, :]).astype(
        jnp.bfloat16
    )
    spread_back = jnp.dot(chooser, returned, preferred_element_type=jnp.float32)
    byte_lengths = jnp.sum(jnp.where(member, lengths[:, None], 0.0), axis=0)
    byte_grad = (spread_back / byte_lengths[:, None]).astype(jnp.bfloat16)
    return (attn_out, byte_grad)


def solution(mesh):
    placed = (P("ctx", None), P("ctx"), P(), P(), P(None, None, "tp"), P("ctx", "tp"))
    return jax.shard_map(
        shards,
        mesh=mesh,
        in_specs=placed,
        out_specs=(P("ctx", "tp"), P("ctx", "tp")),
        check_vma=False,
    )
```

profile of v0, /device:TPU:6, one launch (start us, length us, event | category | flops | bytes accessed | tf_op | source)
XLA Modules:
  0.0 305.7 jit_solution(10949627991634043434)
XLA Ops:
  9.7 3.4 %collective-permute-start = (bf16[128,512]{1,0:T(8,128)(2,1)S(1)}, bf16[128,512]{1,0:T(8,128)(2,1)S(1)}, u32[]{:S(2)}, u32[]{:S(2)}) collective-permute-start(bf16[128,512]{1,0:T(8,128)(2,1)S(1)} %fusion.56), channel_id=1, source_target_pairs={{0,2},{2,4},{4,6},{6,8},{8,10},{10,12},{12,14},{14,16},{16,18},{18... | collective-permute-start | bytes 393224 | tf_op jit(solution)/shard_map/ppermute | solution.py:16
  13.1 2.4 collective-permute-start.1
  25.7 2.7 fusion.66
  28.5 2.7 fusion.60
  31.3 2.7 fusion.63
  35.4 36.0 %all-gather.13.cloned.1.call-done = bf16[1024,1024]{1,0:T(8,128)(2,1)} async-done(((bf16[64,1024]{1,0:T(8,128)(2,1)}), bf16[1024,1024]{1,0:T(8,128)(2,1)}) %all-gather.13.cloned.1.call-update) | async-done | bytes 2097168 | tf_op jit(solution)/shard_map/all_gather | solution.py:115
  71.4 2.9 copy.61
  74.3 59.7 %all-gather.9.cloned.1.call-done = bf16[1024,1024]{1,0:T(8,128)(2,1)} async-done(((bf16[64,1024]{1,0:T(8,128)(2,1)}), bf16[1024,1024]{1,0:T(8,128)(2,1)}) %all-gather.9.cloned.1.call-update) | async-done | bytes 2097168 | tf_op jit(solution)/shard_map/all_gather | solution.py:83
  134.0 2.6 select_reduce_fusion
  138.5 33.8 %all-gather = f32[16,64,8]{1,2,0:T(8,128)S(1)} all-gather(f32[1,64,8]{1,2,0:T(8,128)S(1)} %bitcast.202), channel_id=1, replica_groups=mesh['ctx'=16,'tp'=2] {'ctx'}, dimensions={0}, use_global_device_ids=true | all-gather | bytes 34816 | tf_op jit(solution)/shard_map/all_gather | solution.py:109
  172.4 23.7 %all-gather.7.cloned.1.call-done = bf16[1024,1024]{1,0:T(8,128)(2,1)} async-done(((bf16[64,1024]{1,0:T(8,128)(2,1)}), bf16[1024,1024]{1,0:T(8,128)(2,1)}) %all-gather.7.cloned.1.call-update) | async-done | bytes 2097168 | tf_op jit(solution)/shard_map/all_gather | solution.py:84
  196.2 3.8 %multiply_reduce_fusion = (f32[64,8]{0,1:T(8,128)S(1)}, bf16[8,128,64]{1,2,0:T(8,128)(2,1)}) fusion(f32[8,64,1024]{2,1,0:T(8,128)} %copy-done.2, f32[8,64]{1,0:T(8,128)S(1)} %log_add_fusion, pred[64,1024]{1,0:T(8,128)(4,1)S(1)} %broadcast_compare_fusion.1, bf16[1024,1024]{1,0:T(8,128)(2,1)} %all-gather.7.cloned.1.call-done, bf16[64,1024]{1,0:T(8,128)(2,1)S(1)} %copy-done.6), kind=kOutput, calls=%fused_computation.75 | convolution fusion | flops 136642048 | bytes 4526080 | tf_op jit(solution)/shard_map/hqk,khd->qhd/dot_general | solution.py:96
  200.0 33.9 %all-gather.1 = f32[16,64,8]{1,2,0:T(8,128)S(1)} all-gather(f32[1,64,8]{1,2,0:T(8,128)S(1)} %bitcast.203), channel_id=1, replica_groups=mesh['ctx'=16,'tp'=2] {'ctx'}, dimensions={0}, use_global_device_ids=true | all-gather | bytes 34816 | tf_op jit(solution)/shard_map/all_gather | solution.py:110
  233.9 24.8 %all-gather.11.cloned.1.call-done = bf16[1024,1024]{1,0:T(8,128)(2,1)} async-done(((bf16[64,1024]{1,0:T(8,128)(2,1)}), bf16[1024,1024]{1,0:T(8,128)(2,1)}) %all-gather.11.cloned.1.call-update) | async-done | bytes 2097168 | tf_op jit(solution)/shard_map/all_gather | solution.py:114
  258.7 2.7 select_exponential_fusion
  262.8 3.3 %fusion.75 = bf16[8,8,8,128]{3,2,1,0:T(8,128)(2,1)S(1)} fusion(f32[8,1024,64]{1,2,0:T(8,128)} %copy-done.1, bf16[1024,8,128]{0,2,1:T(8,128)(2,1)S(1)} %bitcast.199, f32[8,1024]{1,0:T(8,128)S(1)} %bitcast.200, bf16[1024,1024]{1,0:T(8,128)(2,1)} %all-gather.11.cloned.1.call-done, bf16[64,1024]{1,0:T(8,128)(2,1)S(1)} %copy-done.4), kind=kOutput, calls=%fused_computation.60 | convolution fusion | flops 270139392 | bytes 6586368 | tf_op jit(solution)/shard_map/hqk,qhd->khd/dot_general | solution.py:133
  266.1 2.5 fusion.14
  268.6 4.0 %fusion.79 = bf16[8,8,8,128]{3,2,1,0:T(8,128)(2,1)S(1)} fusion(f32[8,64,1024]{2,1,0:T(8,128)S(1)} %copy-done.3, f32[8,64]{1,0:T(8,128)S(1)} %bitcast.204, f32[8,64]{1,0:T(8,128)S(1)} %log_add_fusion, pred[64,1024]{1,0:T(8,128)(4,1)S(1)} %broadcast_compare_fusion.1, bf16[1024,1024]{1,0:T(8,128)(2,1)} %all-gather.7.cloned.1.call-done, ...), kind=kOutput, calls=%fused_computation.62 | convolution fusion | flops 271712256 | bytes 6623232 | tf_op jit(solution)/shard_map/hqk,khd->qhd/dot_general | solution.py:105
  272.6 2.4 fusion.47
  275.0 3.1 %fusion.44 = f32[64,1024]{1,0:T(8,128)} fusion(f32[64,1024]{1,0:T(8,128)S(1)} %fusion.47, bf16[3,1024,1024]{2,1,0:T(8,128)(2,1)} %param.10, bf16[8,8,8,128]{3,2,1,0:T(8,128)(2,1)S(1)} %fusion.78), kind=kOutput, calls=%fused_computation.47 | convolution fusion | flops 134283264 | bytes 2752512 | tf_op jit(solution)/shard_map/dot_general | solution.py:144
  283.4 2.6 reduce-scatter.2.cloned.1.call-done
  286.9 3.4 %collective-permute-start.2 = (bf16[64,512]{1,0:T(8,128)(2,1)S(1)}, bf16[64,512]{1,0:T(8,128)(2,1)S(1)}, u32[]{:S(2)}, u32[]{:S(2)}) collective-permute-start(bf16[64,512]{1,0:T(8,128)(2,1)S(1)} %convert_element_type.89), channel_id=1, source_target_pairs={{0,2},{2,4},{4,6},{6,8},{8,10},{10,12},{12,14},{14,16},{16,18},{18... | collective-permute-start | bytes 196616 | tf_op jit(solution)/shard_map/ppermute | solution.py:16
  290.2 2.5 collective-permute-start.3
  293.4 4.8 %collective-permute-done.3 = bf16[64,512]{1,0:T(8,128)(2,1)S(1)} collective-permute-done((bf16[64,512]{1,0:T(8,128)(2,1)S(1)}, bf16[64,512]{1,0:T(8,128)(2,1)S(1)}, u32[]{:S(2)}, u32[]{:S(2)}) %collective-permute-start.3) | collective-permute-done | bytes 65568 | tf_op jit(solution)/shard_map/ppermute | solution.py:17
  (89 shorter events, 22.8 us)
Async XLA Ops:
  7.2 1.6 copy-start
  7.2 64.3 %all-gather.13.cloned.1.call-start = ((), (), s32[]{:S(2)}) async-start(), calls=%async_computation.4 | async-start | bytes 2228224 | tf_op jit(solution)/shard_map/all_gather | solution.py:115
  7.9 126.1 %all-gather.9.cloned.1.call-start = ((), (), s32[]{:S(2)}) async-start(), calls=%async_computation.2 | async-start | bytes 2228224 | tf_op jit(solution)/shard_map/all_gather | solution.py:83
  9.7 13.9 %collective-permute-start = (bf16[128,512]{1,0:T(8,128)(2,1)S(1)}, bf16[128,512]{1,0:T(8,128)(2,1)S(1)}, u32[]{:S(2)}, u32[]{:S(2)}) collective-permute-start(bf16[128,512]{1,0:T(8,128)(2,1)S(1)} %fusion.56), channel_id=1, source_target_pairs={{0,2},{2,4},{4,6},{6,8},{8,10},{10,12},{12,14},{14,16},{16,18},{18... | collective-permute-start | bytes 393224 | tf_op jit(solution)/shard_map/ppermute | solution.py:16
  13.1 10.5 %collective-permute-start.1 = (bf16[128,512]{1,0:T(8,128)(2,1)S(1)}, bf16[128,512]{1,0:T(8,128)(2,1)S(1)}, u32[]{:S(2)}, u32[]{:S(2)}) collective-permute-start(bf16[128,512]{1,0:T(8,128)(2,1)S(1)} %fusion.56), channel_id=1, source_target_pairs={{2,0},{4,2},{6,4},{8,6},{10,8},{12,10},{14,12},{16,14},{18,16},{20... | collective-permute-start | bytes 393224 | tf_op jit(solution)/shard_map/ppermute | solution.py:17
  28.4 167.7 %all-gather.7.cloned.1.call-start = ((), (), s32[]{:S(2)}) async-start(), calls=%async_computation.1 | async-start | bytes 2228224 | tf_op jit(solution)/shard_map/all_gather | solution.py:84
  31.2 3.7 %copy-start.9 = (s32[16]{0:T(128)S(1)}, s32[16]{0:T(128)}, u32[]{:S(2)}) copy-start(s32[16]{0:T(128)} %param.8) | copy-start | bytes 196
  31.2 227.5 %all-gather.11.cloned.1.call-start = ((), (), s32[]{:S(2)}) async-start(), calls=%async_computation.3 | async-start | bytes 2228224 | tf_op jit(solution)/shard_map/all_gather | solution.py:114
  34.0 251.9 %reduce-scatter.2.cloned.1.call-start = ((), (), s32[]{:S(2)}) async-start(), calls=%async_computation.5 | async-start | bytes 393216 | tf_op jit(solution)/shard_map/reduce_scatter | solution.py:147
  35.4 98.6 %copy-start.5 = (bf16[64,1024]{1,0:T(8,128)(2,1)S(1)}, bf16[64,1024]{1,0:T(8,128)(2,1)}, u32[]{:S(2)}) copy-start(bf16[64,1024]{1,0:T(8,128)(2,1)} %fusion.63) | copy-start | bytes 393220
  136.6 1.4 copy-start.2
  136.6 59.6 %copy-start.6 = (bf16[64,1024]{1,0:T(8,128)(2,1)S(1)}, bf16[64,1024]{1,0:T(8,128)(2,1)}, u32[]{:S(2)}) copy-start(bf16[64,1024]{1,0:T(8,128)(2,1)} %param.11) | copy-start | bytes 393220
  172.4 86.3 %copy-start.7 = (bf16[64,1024]{1,0:T(8,128)(2,1)S(1)}, bf16[64,1024]{1,0:T(8,128)(2,1)}, u32[]{:S(2)}) copy-start(bf16[64,1024]{1,0:T(8,128)(2,1)} %fusion.66) | copy-start | bytes 393220
  261.4 1.4 copy-start.1
  261.4 1.4 copy-start.4
  266.1 2.5 copy-start.3
  275.0 7.6 %copy-start.10 = (s32[256]{0:T(256)S(1)}, s32[256]{0:T(256)}, u32[]{:S(2)}) copy-start(s32[256]{0:T(256)} %param.7) | copy-start | bytes 3076
  275.0 17.7 %copy-start.8 = (bf16[8,128,64]{1,2,0:T(8,128)(2,1)S(1)}, bf16[8,128,64]{1,2,0:T(8,128)(2,1)}, u32[]{:S(2)}) copy-start(bf16[8,128,64]{1,2,0:T(8,128)(2,1)} %get-tuple-element.18) | copy-start | bytes 393220
  286.9 6.5 %collective-permute-start.2 = (bf16[64,512]{1,0:T(8,128)(2,1)S(1)}, bf16[64,512]{1,0:T(8,128)(2,1)S(1)}, u32[]{:S(2)}, u32[]{:S(2)}) collective-permute-start(bf16[64,512]{1,0:T(8,128)(2,1)S(1)} %convert_element_type.89), channel_id=1, source_target_pairs={{0,2},{2,4},{4,6},{6,8},{8,10},{10,12},{12,14},{14,16},{16,18},{18... | collective-permute-start | bytes 196616 | tf_op jit(solution)/shard_map/ppermute | solution.py:16
  290.2 8.0 %collective-permute-start.3 = (bf16[64,512]{1,0:T(8,128)(2,1)S(1)}, bf16[64,512]{1,0:T(8,128)(2,1)S(1)}, u32[]{:S(2)}, u32[]{:S(2)}) collective-permute-start(bf16[64,512]{1,0:T(8,128)(2,1)S(1)} %convert_element_type.89), channel_id=1, source_target_pairs={{2,0},{4,2},{6,4},{8,6},{10,8},{12,10},{14,12},{16,14},{18,16},{20... | collective-permute-start | bytes 196616 | tf_op jit(solution)/shard_map/ppermute | solution.py:17
Sparse Core Ops, SparseCore 0:
  10.8 60.6 all-gather.12
  74.8 59.1 all-gather.8
  136.8 59.3 all-gather.6
  199.4 59.2 all-gather.10
  278.3 7.6 reduce-scatter.1
where the time goes:
time: 306 us
  waiting for transfers between devices  152 us (50%)
  blocking collectives  69.5 us (23%)
  matrix products  35.5 us (12%)
  between operations  16.7 us (5%)
  local copies, waits for them, and re-layouts  13.3 us (4%)
  starting transfers between devices  11.9 us (4%)
  other arithmetic  6.49 us (2%)
    all_gather x1, waiting for transfers between devices, shards(): lax.all_gather(keyed, 'ctx', axis=0, tiled=True)  59.7 us
    all_gather x1, waiting for transfers between devices, shards(): g_piece = lax.all_gather(d_attn, 'ctx', axis=0, tiled=True)  36 us
    all_gather x1, blocking collectives, shards(): lax.all_gather(delta, 'ctx', axis=0, tiled=True)  33.9 us
    all_gather x1, blocking collectives, shards(): lax.all_gather(lse_rows, 'ctx', axis=0, tiled=True)  33.8 us
    all_gather x1, waiting for transfers between devices, shards(): q_piece = lax.all_gather(query, 'ctx', axis=0, tiled=True)  24.8 us
    all_gather x1, waiting for transfers between devices, shards(): lax.all_gather(valued, 'ctx', axis=0, tiled=True)  23.7 us
    ppermute x2, starting transfers between devices, extended_2(): before = lax.ppermute(last, axis, up)  6.77 us
  transfers between devices with their start and end apart: 9, of which 6 were waited for; matrix products, arithmetic and copies ran while one was open for 11% of the time, Pallas kernels for 0%

commit v1 on v0

--- a/solution.py
+++ b/solution.py
@@ -4,6 +4,18 @@
 from jax.sharding import PartitionSpec as P
 
 HD = 128
+
+
+def doubled_up(array, axis, dim):
+    ways, here = (lax.axis_size(axis), lax.axis_index(axis))
+    grown, reach = (array, 1)
+    while reach < ways:
+        theirs = lax.ppermute(grown, axis, [(d, d ^ reach) for d in range(ways)])
+        mine_first = jnp.concatenate([grown, theirs], axis=dim)
+        theirs_first = jnp.concatenate([theirs, grown], axis=dim)
+        grown = jnp.where(here & reach == 0, mine_first, theirs_first)
+        reach = 2 * reach
+    return grown
 
 
 def extended_2(x, sides, width):
@@ -81,7 +93,7 @@
     valued = jnp.dot(pooled, w_qkv[2], preferred_element_type=jnp.float32).astype(jnp.bfloat16)
     keys_all, values_all = (
         lax.all_gather(keyed, "ctx", axis=0, tiled=True),
-        lax.all_gather(valued, "ctx", axis=0, tiled=True),
+        doubled_up(valued, "ctx", 0),
     )
     query3 = query.reshape(rows, heads, HD)
     keys3 = keys_all.reshape(total, heads, HD)

time: 306 us -> 295 us (0.964)
  waiting for transfers between devices: 152 us -> 124 us
  starting transfers between devices: 11.9 us -> 18.2 us
  blocking collectives: 69.5 us -> 75 us
    ppermute x0 -> x4, waiting for transfers between devices: none -> 75.2 us  [doubled_up(): theirs = lax.ppermute(grown, axis, [(d, d ^ reach) for d in range(ways)])]
    all_gather x1, waiting for transfers between devices: 36 us -> 0.01 us  [shards(): g_piece = lax.all_gather(d_attn, 'ctx', axis=0, tiled=True)]
    all_gather x1, waiting for transfers between devices: 24.8 us -> 0.01 us  [shards(): q_piece = lax.all_gather(query, 'ctx', axis=0, tiled=True)]
    all_gather x1 -> x0, waiting for transfers between devices: 23.7 us -> none  [shards(): lax.all_gather(valued, 'ctx', axis=0, tiled=True)]
    all_gather x1, waiting for transfers between devices: 59.7 us -> 39.4 us  [shards(): lax.all_gather(keyed, 'ctx', axis=0, tiled=True)]
    ppermute x0 -> x4, starting transfers between devices: none -> 6.37 us  [doubled_up(): theirs = lax.ppermute(grown, axis, [(d, d ^ reach) for d in range(ways)])]
    all_gather x1, blocking collectives: 33.9 us -> 39.4 us  [shards(): lax.all_gather(delta, 'ctx', axis=0, tiled=True)]
  transfers between devices with their start and end apart: 9 -> 12, of which waited for: 6 -> 7; matrix products, arithmetic and copies ran while one was open for 11% -> 12% of each run, Pallas kernels for 0% -> 0%
where the time goes in v1:
time: 295 us; the launch traced here: 294 us
  waiting for transfers between devices  124 us (42%)
  blocking collectives  75 us (25%)
  matrix products  36.8 us (12%)
  starting transfers between devices  18.2 us (6%)
  between operations  16.7 us (6%)
  local copies, waits for them, and re-layouts  14.8 us (5%)
  other arithmetic  8.51 us (3%)
    ppermute x4, waiting for transfers between devices, doubled_up(): theirs = lax.ppermute(grown, axis, [(d, d ^ reach) for d in range(ways)])  75.2 us
    all_gather x1, waiting for transfers between devices, shards(): lax.all_gather(keyed, 'ctx', axis=0, tiled=True)  39.4 us
    all_gather x1, blocking collectives, shards(): lax.all_gather(delta, 'ctx', axis=0, tiled=True)  39.4 us
    all_gather x1, blocking collectives, shards(): lax.all_gather(lse_rows, 'ctx', axis=0, tiled=True)  33.8 us
    ppermute x2, starting transfers between devices, extended_2(): before = lax.ppermute(last, axis, up)  6.78 us
    ppermute x4, starting transfers between devices, doubled_up(): theirs = lax.ppermute(grown, axis, [(d, d ^ reach) for d in range(ways)])  6.37 us
  transfers between devices with their start and end apart: 12, of which 7 were waited for; matrix products, arithmetic and copies ran while one was open for 12% of the time, Pallas kernels for 0%

profile of v1, /device:TPU:6, one launch (start us, length us, event | category | flops | bytes accessed | tf_op | source)
XLA Modules:
  0.0 294.1 jit_solution(3506044260968562523)
XLA Ops:
  9.7 3.4 %collective-permute-start = (bf16[128,512]{1,0:T(8,128)(2,1)S(1)}, bf16[128,512]{1,0:T(8,128)(2,1)S(1)}, u32[]{:S(2)}, u32[]{:S(2)}) collective-permute-start(bf16[128,512]{1,0:T(8,128)(2,1)S(1)} %fusion.48), channel_id=1, source_target_pairs={{0,2},{2,4},{4,6},{6,8},{8,10},{10,12},{12,14},{14,16},{16,18},{18... | collective-permute-start | bytes 393224 | tf_op jit(solution)/shard_map/ppermute | solution.py:28
  13.1 2.4 collective-permute-start.1
  25.7 2.7 fusion.58
  32.1 2.7 fusion.55
  37.9 7.8 %collective-permute-done.3 = bf16[128,1024]{1,0:T(8,128)(2,1)S(1)} collective-permute-done((bf16[128,1024]{1,0:T(8,128)(2,1)S(1)}, bf16[128,1024]{1,0:T(8,128)(2,1)S(1)}, u32[]{:S(2)}, u32[]{:S(2)}) %collective-permute-start.3) | collective-permute-done | bytes 262176 | tf_op jit(solution)/shard_map/ppermute | solution.py:13
  47.7 18.3 %collective-permute-done.4 = bf16[256,1024]{1,0:T(8,128)(2,1)S(1)} collective-permute-done((bf16[256,1024]{1,0:T(8,128)(2,1)S(1)}, bf16[256,1024]{1,0:T(8,128)(2,1)S(1)}, u32[]{:S(2)}, u32[]{:S(2)}) %collective-permute-start.4) | collective-permute-done | bytes 524320 | tf_op jit(solution)/shard_map/ppermute | solution.py:13
  66.5 2.7 collective-permute-start.5
  71.0 47.8 %collective-permute-done.5 = bf16[512,1024]{1,0:T(8,128)(2,1)S(1)} collective-permute-done((bf16[512,1024]{1,0:T(8,128)(2,1)S(1)}, bf16[512,1024]{1,0:T(8,128)(2,1)S(1)}, u32[]{:S(2)}, u32[]{:S(2)}) %collective-permute-start.5) | collective-permute-done | bytes 1048608 | tf_op jit(solution)/shard_map/ppermute | solution.py:13
  120.0 2.9 copy.95
  122.9 39.4 %all-gather.6.cloned.1.call-done = bf16[1024,1024]{1,0:T(8,128)(2,1)} async-done(((bf16[64,1024]{1,0:T(8,128)(2,1)}), bf16[1024,1024]{1,0:T(8,128)(2,1)}) %all-gather.6.cloned.1.call-update) | async-done | bytes 2097168 | tf_op jit(solution)/shard_map/all_gather | solution.py:95
  162.3 2.6 select_reduce_fusion
  166.8 33.8 %all-gather = f32[16,64,8]{1,2,0:T(8,128)S(1)} all-gather(f32[1,64,8]{1,2,0:T(8,128)S(1)} %bitcast.203), channel_id=1, replica_groups=mesh['ctx'=16,'tp'=2] {'ctx'}, dimensions={0}, use_global_device_ids=true | all-gather | bytes 34816 | tf_op jit(solution)/shard_map/all_gather | solution.py:121
  200.7 4.9 %multiply_reduce_fusion = (f32[64,8]{0,1:T(8,128)S(1)}, bf16[8,128,64]{1,2,0:T(8,128)(2,1)}) fusion(bf16[512,8,128]{2,0,1:T(8,128)(2,1)} %copy_bitcast_fusion, bf16[512,8,128]{2,0,1:T(8,128)(2,1)} %maximum_select_fusion.1, pred[]{:T(512)S(6)} %eq.53, f32[8,64,1024]{2,1,0:T(8,128)} %copy-done.2, f32[8,64]{1,0:T(8,128)S(1)} %log_add_fusion, ...), kind=kOutput, calls=%fused_computation.79 | convolution fusion | flops 146079232 | bytes 4526081 | tf_op jit(solution)/shard_map/hqk,khd->qhd/dot_general | solution.py:108
  205.6 39.4 %all-gather.1 = f32[16,64,8]{1,2,0:T(8,128)S(1)} all-gather(f32[1,64,8]{1,2,0:T(8,128)S(1)} %bitcast.204), channel_id=1, replica_groups=mesh['ctx'=16,'tp'=2] {'ctx'}, dimensions={0}, use_global_device_ids=true | all-gather | bytes 34816 | tf_op jit(solution)/shard_map/all_gather | solution.py:122
  245.1 2.7 select_exponential_fusion
  249.2 3.3 %fusion.64 = bf16[8,8,8,128]{3,2,1,0:T(8,128)(2,1)S(1)} fusion(f32[8,1024,64]{1,2,0:T(8,128)} %copy-done.1, bf16[1024,8,128]{0,2,1:T(8,128)(2,1)S(1)} %bitcast.200, f32[8,1024]{1,0:T(8,128)S(1)} %bitcast.201, bf16[1024,1024]{1,0:T(8,128)(2,1)} %all-gather.8.cloned.1.call-done, bf16[64,1024]{1,0:T(8,128)(2,1)S(1)} %fusion.52), kind=kOutput, calls=%fused_computation.55 | convolution fusion | flops 270139392 | bytes 6586368 | tf_op jit(solution)/shard_map/hqk,qhd->khd/dot_general | solution.py:145
  252.6 2.5 fusion.10
  255.1 4.9 %fusion.68 = bf16[8,8,8,128]{3,2,1,0:T(8,128)(2,1)S(1)} fusion(f32[8,64,1024]{2,1,0:T(8,128)S(1)} %copy-done.3, f32[8,64]{1,0:T(8,128)S(1)} %bitcast.205, f32[8,64]{1,0:T(8,128)S(1)} %log_add_fusion, pred[64,1024]{1,0:T(8,128)(4,1)S(1)} %broadcast_compare_fusion.1, bf16[512,8,128]{2,0,1:T(8,128)(2,1)} %copy_bitcast_fusion, ...), kind=kOutput, calls=%fused_computation.57 | convolution fusion | flops 281149440 | bytes 6623233 | tf_op jit(solution)/shard_map/hqk,khd->qhd/dot_general | solution.py:117
  259.9 2.4 fusion.39
  262.3 3.1 %fusion.36 = f32[64,1024]{1,0:T(8,128)} fusion(f32[64,1024]{1,0:T(8,128)S(1)} %fusion.39, bf16[3,1024,1024]{2,1,0:T(8,128)(2,1)} %param.10, bf16[8,8,8,128]{3,2,1,0:T(8,128)(2,1)S(1)} %fusion.67), kind=kOutput, calls=%fused_computation.42 | convolution fusion | flops 134283264 | bytes 2752512 | tf_op jit(solution)/shard_map/dot_general | solution.py:156
  270.5 3.8 %reduce-scatter.2.cloned.1.call-done = f32[64,512]{1,0:T(8,128)} async-done(((f32[64,1024]{1,0:T(8,128)}), f32[64,512]{1,0:T(8,128)}) %reduce-scatter.2.cloned.1.call-update) | async-done | bytes 131088 | tf_op jit(solution)/shard_map/reduce_scatter | solution.py:159
  275.3 3.4 %collective-permute-start.6 = (bf16[64,512]{1,0:T(8,128)(2,1)S(1)}, bf16[64,512]{1,0:T(8,128)(2,1)S(1)}, u32[]{:S(2)}, u32[]{:S(2)}) collective-permute-start(bf16[64,512]{1,0:T(8,128)(2,1)S(1)} %convert_element_type.89), channel_id=1, source_target_pairs={{0,2},{2,4},{4,6},{6,8},{8,10},{10,12},{12,14},{14,16},{16,18},{18... | collective-permute-start | bytes 196616 | tf_op jit(solution)/shard_map/ppermute | solution.py:28
  278.6 2.5 collective-permute-start.7
  281.8 4.8 %collective-permute-done.7 = bf16[64,512]{1,0:T(8,128)(2,1)S(1)} collective-permute-done((bf16[64,512]{1,0:T(8,128)(2,1)S(1)}, bf16[64,512]{1,0:T(8,128)(2,1)S(1)}, u32[]{:S(2)}, u32[]{:S(2)}) %collective-permute-start.7) | collective-permute-done | bytes 65568 | tf_op jit(solution)/shard_map/ppermute | solution.py:29
  (105 shorter events, 33.3 us)
Async XLA Ops:
  7.2 1.6 copy-start
  7.2 112.8 %all-gather.10.cloned.1.call-start = ((), (), s32[]{:S(2)}) async-start(), calls=%async_computation.3 | async-start | bytes 2228224 | tf_op jit(solution)/shard_map/all_gather | solution.py:127
  7.9 154.4 %all-gather.6.cloned.1.call-start = ((), (), s32[]{:S(2)}) async-start(), calls=%async_computation.1 | async-start | bytes 2228224 | tf_op jit(solution)/shard_map/all_gather | solution.py:95
  9.7 13.9 %collective-permute-start = (bf16[128,512]{1,0:T(8,128)(2,1)S(1)}, bf16[128,512]{1,0:T(8,128)(2,1)S(1)}, u32[]{:S(2)}, u32[]{:S(2)}) collective-permute-start(bf16[128,512]{1,0:T(8,128)(2,1)S(1)} %fusion.48), channel_id=1, source_target_pairs={{0,2},{2,4},{4,6},{6,8},{8,10},{10,12},{12,14},{14,16},{16,18},{18... | collective-permute-start | bytes 393224 | tf_op jit(solution)/shard_map/ppermute | solution.py:28
  13.1 10.5 %collective-permute-start.1 = (bf16[128,512]{1,0:T(8,128)(2,1)S(1)}, bf16[128,512]{1,0:T(8,128)(2,1)S(1)}, u32[]{:S(2)}, u32[]{:S(2)}) collective-permute-start(bf16[128,512]{1,0:T(8,128)(2,1)S(1)} %fusion.48), channel_id=1, source_target_pairs={{2,0},{4,2},{6,4},{8,6},{10,8},{12,10},{14,12},{16,14},{18,16},{20... | collective-permute-start | bytes 393224 | tf_op jit(solution)/shard_map/ppermute | solution.py:29
  28.5 216.7 %all-gather.8.cloned.1.call-start = ((), (), s32[]{:S(2)}) async-start(), calls=%async_computation.2 | async-start | bytes 2228224 | tf_op jit(solution)/shard_map/all_gather | solution.py:126
  30.6 7.1 %copy-start.9 = (s32[16]{0:T(128)S(1)}, s32[16]{0:T(128)}, u32[]{:S(2)}) copy-start(s32[16]{0:T(128)} %param.8) | copy-start | bytes 196
  30.6 5.6 %collective-permute-start.2 = (bf16[64,1024]{1,0:T(8,128)(2,1)S(1)}, bf16[64,1024]{1,0:T(8,128)(2,1)S(1)}, u32[]{:S(2)}, u32[]{:S(2)}) collective-permute-start(bf16[64,1024]{1,0:T(8,128)(2,1)S(1)} %fusion.52), channel_id=1, source_target_pairs={{0,2},{2,0},{4,6},{6,4},{8,10},{10,8},{12,14},{14,12},{16,18},{18,... | collective-permute-start | bytes 393224 | tf_op jit(solution)/shard_map/ppermute | solution.py:13
  34.8 239.5 %reduce-scatter.2.cloned.1.call-start = ((), (), s32[]{:S(2)}) async-start(), calls=%async_computation.4 | async-start | bytes 393216 | tf_op jit(solution)/shard_map/reduce_scatter | solution.py:159
  36.3 9.4 %collective-permute-start.3 = (bf16[128,1024]{1,0:T(8,128)(2,1)S(1)}, bf16[128,1024]{1,0:T(8,128)(2,1)S(1)}, u32[]{:S(2)}, u32[]{:S(2)}) collective-permute-start(bf16[128,1024]{1,0:T(8,128)(2,1)S(1)} %maximum_select_fusion.9), channel_id=1, source_target_pairs={{0,4},{2,6},{4,0},{6,2},{8,12},{10,14},{12,8},{14,10},{16,20},{18,... | collective-permute-start | bytes 786440 | tf_op jit(solution)/shard_map/ppermute | solution.py:13
  45.9 20.2 %collective-permute-start.4 = (bf16[256,1024]{1,0:T(8,128)(2,1)S(1)}, bf16[256,1024]{1,0:T(8,128)(2,1)S(1)}, u32[]{:S(2)}, u32[]{:S(2)}) collective-permute-start(bf16[256,1024]{1,0:T(8,128)(2,1)S(1)} %maximum_select_fusion.4), channel_id=1, source_target_pairs={{0,8},{2,10},{4,12},{6,14},{8,0},{10,2},{12,4},{14,6},{16,24},{18,... | collective-permute-start | bytes 1572872 | tf_op jit(solution)/shard_map/ppermute | solution.py:13
  66.5 52.2 %collective-permute-start.5 = (bf16[512,1024]{1,0:T(8,128)(2,1)S(1)}, bf16[512,1024]{1,0:T(8,128)(2,1)S(1)}, u32[]{:S(2)}, u32[]{:S(2)}) collective-permute-start(bf16[512,1024]{1,0:T(8,128)(2,1)S(1)} %maximum_select_fusion.2), channel_id=1, source_target_pairs={{0,16},{2,18},{4,20},{6,22},{8,24},{10,26},{12,28},{14,30},{16,0},... | collective-permute-start | bytes 3145736 | tf_op jit(solution)/shard_map/ppermute | solution.py:13
  120.0 42.3 %copy-start.4 = (bf16[64,1024]{1,0:T(8,128)(2,1)S(1)}, bf16[64,1024]{1,0:T(8,128)(2,1)}, u32[]{:S(2)}) copy-start(bf16[64,1024]{1,0:T(8,128)(2,1)} %fusion.55) | copy-start | bytes 393220
  164.9 1.3 copy-start.2
  164.9 35.8 %copy-start.5 = (bf16[64,1024]{1,0:T(8,128)(2,1)S(1)}, bf16[64,1024]{1,0:T(8,128)(2,1)}, u32[]{:S(2)}) copy-start(bf16[64,1024]{1,0:T(8,128)(2,1)} %param.11) | copy-start | bytes 393220
  200.7 44.4 %copy-start.7 = (bf16[64,1024]{1,0:T(8,128)(2,1)S(1)}, bf16[64,1024]{1,0:T(8,128)(2,1)}, u32[]{:S(2)}) copy-start(bf16[64,1024]{1,0:T(8,128)(2,1)} %fusion.58) | copy-start | bytes 393220
  247.8 1.4 copy-start.1
  252.5 2.5 copy-start.3
  252.5 2.5 copy-start.6
  262.3 7.5 %copy-start.10 = (s32[256]{0:T(256)S(1)}, s32[256]{0:T(256)}, u32[]{:S(2)}) copy-start(s32[256]{0:T(256)} %param.7) | copy-start | bytes 3076
  262.3 18.8 %copy-start.8 = (bf16[8,128,64]{1,2,0:T(8,128)(2,1)S(1)}, bf16[8,128,64]{1,2,0:T(8,128)(2,1)}, u32[]{:S(2)}) copy-start(bf16[8,128,64]{1,2,0:T(8,128)(2,1)} %get-tuple-element.18) | copy-start | bytes 393220
  275.3 6.5 %collective-permute-start.6 = (bf16[64,512]{1,0:T(8,128)(2,1)S(1)}, bf16[64,512]{1,0:T(8,128)(2,1)S(1)}, u32[]{:S(2)}, u32[]{:S(2)}) collective-permute-start(bf16[64,512]{1,0:T(8,128)(2,1)S(1)} %convert_element_type.89), channel_id=1, source_target_pairs={{0,2},{2,4},{4,6},{6,8},{8,10},{10,12},{12,14},{14,16},{16,18},{18... | collective-permute-start | bytes 196616 | tf_op jit(solution)/shard_map/ppermute | solution.py:28
  278.6 8.0 %collective-permute-start.7 = (bf16[64,512]{1,0:T(8,128)(2,1)S(1)}, bf16[64,512]{1,0:T(8,128)(2,1)S(1)}, u32[]{:S(2)}, u32[]{:S(2)}) collective-permute-start(bf16[64,512]{1,0:T(8,128)(2,1)S(1)} %convert_element_type.89), channel_id=1, source_target_pairs={{2,0},{4,2},{6,4},{8,6},{10,8},{12,10},{14,12},{16,14},{18,16},{20... | collective-permute-start | bytes 196616 | tf_op jit(solution)/shard_map/ppermute | solution.py:29
Sparse Core Ops, SparseCore 0:
  10.8 86.3 all-gather.9
  100.5 61.7 all-gather.5
  165.6 59.5 all-gather.7
  265.5 8.7 reduce-scatter.1
